TPU v7x, 32 devices: a whole 2x2x4 slice. The times are simulated.
32 devices in a mesh: shard: 8 (over z, y), model: 4 (over x, core).
Axes of the slice: x: 2, y: 2, z: 4, core: 2. Of those that a mesh axis runs over, the one named last changes fastest.
Arguments:
- gradients: float32 [32, 128, 4096], P(None, 'shard', 'model'), may hold values from -6 to 6
- momentum: float32 [32, 128, 4096], P(None, 'shard', 'model'), may hold values from -6 to 6
- weights: float32 [32, 128, 4096], P(None, 'shard', 'model'), may hold values from -0.1875 to 0.1875
Outputs:
- new_weights: float32 [32, 128, 4096], P(None, 'shard', 'model')
- new_momentum: float32 [32, 128, 4096], P(None, 'shard', 'model')
All inputs are finite; a program needn't handle non-finite values.
Results may differ from a plain program's by a relative error of at most 0.00015.
Values sent between devices are 32-bit elements; how exact they have to be, the bound alone decides.
A program may use at most 128 MiB of HBM per device.

v0:
```python
import functools

import jax
import jax.numpy as jnp
from jax import lax
from jax.experimental import pallas as pl
from jax.experimental.pallas import tpu as pltpu
from jax.sharding import PartitionSpec as P

ITERS = 4
VMEM_LIMIT = 40 * 1024 * 1024
FINISH_LIMIT = 16 * 1024 * 1024
MESH = pl.DeviceIdType.MESH
HIGHEST = lax.Precision.HIGHEST


hold_rate = 0.8
learn_rate = 1.0


def mm(a, b):
    return jnp.dot(a, b, precision=HIGHEST, preferred_element_type=jnp.float32)


def direction(gram):
    side = gram.shape[-1]
    row = lax.broadcasted_iota(jnp.int32, (side, side), 0)
    col = lax.broadcasted_iota(jnp.int32, (side, side), 1)
    diagonal = row == col
    squares = jnp.sum(jnp.where(diagonal, gram, 0.0), axis=(0, 1), keepdims=True)
    scale = lax.rsqrt(squares + 1e-06)
    a = gram * scale * scale
    q = jnp.where(diagonal, jnp.broadcast_to(scale, gram.shape), 0.0)
    for step in range(ITERS):
        mixed = -4.775 * a + 2.0315 * mm(a, a)
        if step == 0:
            q_next = 3.4445 * q + mixed * scale
        else:
            q_next = 3.4445 * q + mm(mixed, q)
        if step < ITERS - 1:
            half = 3.4445 * a + mm(mixed, a)
            a = 3.4445 * half + mm(mixed, half)
        q = q_next
    return q


def partner(me, off, n):
    if n & (n - 1):
        return lax.rem(me + off, n)
    for bit in range(n.bit_length() - 1):
        if (off >> bit) & 1:
            me = me + (1 - 2 * ((me // (1 << bit)) % 2)) * (1 << bit)
    return me


def exchange_kernel(n, k, g_ref, m_ref, back_ref, new_ref, grad, moved, held, result, grams,
                    l_grad, l_moved, f_send, f_recv, g_send, g_recv, b_send, b_recv,
                    own_in, own_out, own_new):
    me = lax.axis_index("shard")
    col = lax.axis_index("model")
    local, _, rows, wide = held.shape
    side = n * rows

    def chunk(j):
        return pl.ds(j * n, n)

    def load_grad(j):
        return pltpu.make_async_copy(g_ref.at[chunk(j)], grad.at[j], l_grad.at[j])

    def load_moved(j):
        return pltpu.make_async_copy(m_ref.at[chunk(j)], moved.at[j], l_moved.at[j])

    def store_new(j):
        return pltpu.make_async_copy(moved.at[j], new_ref.at[chunk(j)], own_new.at[j])

    def forward(j, off):
        to = partner(me, off, n)
        return pltpu.make_async_remote_copy(
            src_ref=moved.at[j, to], dst_ref=held.at[j, me],
            send_sem=f_send.at[j, off], recv_sem=f_recv.at[j, off],
            device_id={"shard": to}, device_id_type=MESH)

    def share(j, off):
        return pltpu.make_async_remote_copy(
            src_ref=grams.at[j, col], dst_ref=grams.at[j, col],
            send_sem=g_send.at[j, off], recv_sem=g_recv.at[j, off],
            device_id={"model": partner(col, off, k)}, device_id_type=MESH)

    def backward(j, off):
        to = partner(me, off, n)
        return pltpu.make_async_remote_copy(
            src_ref=result.at[j, to], dst_ref=back_ref.at[j * n + me],
            send_sem=b_send.at[j, off], recv_sem=b_recv.at[j, off],
            device_id={"shard": to}, device_id_type=MESH)

    def mine_in(j):
        return pltpu.make_async_copy(moved.at[j, me], held.at[j, me], own_in.at[j])

    def mine_out(j):
        return pltpu.make_async_copy(result.at[j, me], back_ref.at[j * n + me], own_out.at[j])

    barrier = pltpu.get_barrier_semaphore()
    for off in range(n - 1, 0, -1):
        pl.semaphore_signal(barrier, inc=1, device_id={"shard": partner(me, off, n)}, device_id_type=MESH)
    for off in range(1, k):
        pl.semaphore_signal(barrier, inc=1, device_id={"model": partner(col, off, k)}, device_id_type=MESH)

    @pl.loop(0, local)
    def _(j):
        load_moved(j).start()
        load_grad(j).start()

    def step(j):
        load_moved(j).wait()
        load_grad(j).wait()
        moved[j] = hold_rate * moved[j] + grad[j]

    def send(j):
        for off in range(1, n):
            forward(j, off).start()
        mine_in(j).start()

    step(0)
    pl.semaphore_wait(barrier, n + k - 2)
    send(0)

    @pl.loop(1, local)
    def _(j):
        step(j)
        send(j)

    @pl.loop(0, local)
    def _(j):
        store_new(j).start()

    @pl.loop(0, local)
    def _(j):
        for off in range(1, n):
            forward(j, off).wait_recv()
        mine_in(j).wait()
        x = held[j].reshape(side, wide)
        grams[j, col] = lax.dot_general(
            x, x, (((1,), (1,)), ((), ())), precision=HIGHEST, preferred_element_type=jnp.float32)
        for off in range(1, k):
            share(j, off).start()
        for off in range(1, k):
            share(j, off).wait_recv()
        gram = grams[j, 0]
        for i in range(1, k):
            gram = gram + grams[j, i]
        result[j] = mm(direction(gram), x).reshape(n, rows, wide)
        for off in range(1, n):
            backward(j, off).start()
        mine_out(j).start()

    @pl.loop(0, local)
    def _(j):
        for off in range(1, n):
            forward(j, off).wait_send()
        for off in range(1, k):
            share(j, off).wait_send()
        store_new(j).wait()
        mine_out(j).wait()

    @pl.loop(0, local)
    def _(j):
        for off in range(1, n):
            backward(j, off).wait()


def by_kernel(n, k, gradients, momentum):
    mats, rows, wide = gradients.shape
    local = mats // n
    side = n * rows
    dma = pltpu.SemaphoreType.DMA
    whole = jax.ShapeDtypeStruct(gradients.shape, jnp.float32)
    return pl.pallas_call(
        functools.partial(exchange_kernel, n, k),
        out_shape=(whole, whole),
        in_specs=[pl.BlockSpec(memory_space=pltpu.HBM)] * 2,
        out_specs=[pl.BlockSpec(memory_space=pl.ANY)] * 2,
        scratch_shapes=[
            *[pltpu.VMEM((local, n, rows, wide), jnp.float32)] * 4,
            pltpu.VMEM((local, k, side, side), jnp.float32),
            dma((local,)), dma((local,)),
            dma((local, n)), dma((local, n)),
            dma((local, k)), dma((local, k)),
            dma((local, n)), dma((local, n)),
            dma((local,)), dma((local,)), dma((local,)),
        ],
        compiler_params=pltpu.CompilerParams(
            collective_id=0, has_side_effects=True, vmem_limit_bytes=VMEM_LIMIT),
    )(pltpu.with_memory_space_constraint(gradients, pltpu.HBM), pltpu.with_memory_space_constraint(momentum, pltpu.HBM))


def finish_kernel(pieces, back_ref, w_ref, new_ref, out_w, out_new, done, sem_w, sem_new):
    step = back_ref.shape[0] // pieces

    def part(i):
        return pl.ds(i * step, step)

    def put_new(i):
        return pltpu.make_async_copy(new_ref.at[part(i)], out_new.at[part(i)], sem_new.at[i])

    def put_w(i):
        return pltpu.make_async_copy(done.at[part(i)], out_w.at[part(i)], sem_w.at[i])

    for i in range(pieces):
        put_new(i).start()
    for i in range(pieces):
        done[part(i)] = w_ref[part(i)] - learn_rate * back_ref[part(i)]
        put_w(i).start()
    for i in range(pieces):
        put_new(i).wait()
        put_w(i).wait()


def finish(pieces, back, weights, new_momentum):
    whole = jax.ShapeDtypeStruct(back.shape, jnp.float32)
    hold = pl.BlockSpec(memory_space=pltpu.VMEM)
    leave = pl.BlockSpec(memory_space=pl.ANY)
    return pl.pallas_call(
        functools.partial(finish_kernel, pieces),
        out_shape=(whole, whole),
        in_specs=[hold, hold, leave],
        out_specs=[leave, leave],
        scratch_shapes=[
            pltpu.VMEM(back.shape, jnp.float32),
            pltpu.SemaphoreType.DMA((pieces,)), pltpu.SemaphoreType.DMA((pieces,)),
        ],
        compiler_params=pltpu.CompilerParams(vmem_limit_bytes=FINISH_LIMIT),
        cost_estimate=pl.CostEstimate(flops=2 * back.size, bytes_accessed=20 * back.size, transcendentals=0),
    )(back, weights, new_momentum)


def on_device(n, k, gradients, momentum, weights):
    back, new_momentum = by_kernel(n, k, gradients, momentum)
    return tuple(finish(n, back, weights, new_momentum))


def solution(mesh):
    placed = P(None, "shard", "model")
    return jax.shard_map(
        functools.partial(on_device, mesh.shape["shard"], mesh.shape["model"]),
        mesh=mesh,
        in_specs=(placed, placed, placed),
        out_specs=(placed, placed),
        check_vma=False,
    )
```

profile of v0, /device:TPU:9, one launch (start us, length us, event | category | flops | bytes accessed | tf_op | source)
XLA Modules:
  0.0 99.3 jit_solution(14722909004781523782)
XLA Ops:
  0.6 0.0 copy-start
  0.6 96.5 %shard_map.50 = (f32[32,16,1024]{2,1,0:T(8,128)S(1)}, f32[32,16,1024]{2,1,0:T(8,128)S(1)}) custom-call(f32[32,16,1024]{2,1,0:T(8,128)} %g_ref.1, f32[32,16,1024]{2,1,0:T(8,128)} %m_ref.1), custom_call_target="tpu_custom_call" | custom-call | tf_op jit(solution)/shard_map/pallas_call | solution.py:177
  97.2 0.0 copy-done
  97.2 2.1 %shard_map.51 = (f32[32,16,1024]{2,1,0:T(8,128)}, f32[32,16,1024]{2,1,0:T(8,128)}) custom-call(f32[32,16,1024]{2,1,0:T(8,128)S(1)} %get-tuple-element.4.back_ref, f32[32,16,1024]{2,1,0:T(8,128)S(1)} %copy-done, f32[32,16,1024]{2,1,0:T(8,128)S(1)} %get-tuple-element.5.new_ref), custom_call_target="tpu_custom_call" | custom-call | flops 1048576 | bytes 10485760 | tf_op jit(solution)/shard_map/pallas_call | solution.py:222
Async XLA Ops:
  0.6 96.5 %copy-start = (f32[32,16,1024]{2,1,0:T(8,128)S(1)}, f32[32,16,1024]{2,1,0:T(8,128)}, u32[]{:S(2)}) copy-start(f32[32,16,1024]{2,1,0:T(8,128)} %w_ref.1) | copy-start | bytes 6291460
where the time goes:
time: 100 us; the launch traced here: 99.3 us
  Pallas kernels  98.6 us (99%)
    pallas_call x1, Pallas kernels, by_kernel(): pl.pallas_call(functools.partial(exchange_kernel, n, k), out_shape=(whole...  96.5 us
    pallas_call x1, Pallas kernels, finish(): pl.pallas_call(functools.partial(finish_kernel, pieces), out_shape=(whole...  2.13 us

commit v1 on v0

--- a/solution.py
+++ b/solution.py
@@ -53,13 +53,34 @@
     return me
 
 
+def partners(me, n):
+    offs = range(n - 1, 0, -1)
+    if n & (n - 1) or n < 8:
+        return [(off, partner(me, off, n)) for off in offs]
+    high, next_high = me // (n // 2), me // (n // 4) % 2
+    inner = lax.rem(high + next_high, 2)
+    found = []
+    for off in offs:
+        if off < n // 2:
+            found.append((off, partner(me, off, n)))
+        else:
+            other = off ^ (n // 4)
+            found.append((off + inner * (other - off),
+                          partner(me, off, n) + inner * (partner(me, other, n) - partner(me, off, n))))
+    return found
+
+
 def exchange_kernel(n, k, g_ref, m_ref, back_ref, new_ref, grad, moved, held, result, grams,
                     l_grad, l_moved, f_send, f_recv, g_send, g_recv, b_send, b_recv,
-                    own_in, own_out, own_new):
+                    own_in, own_out, own_new, met, go):
     me = lax.axis_index("shard")
     col = lax.axis_index("model")
     local, _, rows, wide = held.shape
     side = n * rows
+    early = n >= 8 and n & (n - 1) == 0
+    middle = jnp.logical_and(me >= n // 2 - 2, me <= n // 2 + 1)
+    hub = me == 0
+    facing = (n - 1, n - 2)
 
     def chunk(j):
         return pl.ds(j * n, n)
@@ -73,8 +94,7 @@
     def store_new(j):
         return pltpu.make_async_copy(moved.at[j], new_ref.at[chunk(j)], own_new.at[j])
 
-    def forward(j, off):
-        to = partner(me, off, n)
+    def forward(j, off, to):
         return pltpu.make_async_remote_copy(
             src_ref=moved.at[j, to], dst_ref=held.at[j, me],
             send_sem=f_send.at[j, off], recv_sem=f_recv.at[j, off],
@@ -86,8 +106,7 @@
             send_sem=g_send.at[j, off], recv_sem=g_recv.at[j, off],
             device_id={"model": partner(col, off, k)}, device_id_type=MESH)
 
-    def backward(j, off):
-        to = partner(me, off, n)
+    def backward(j, off, to):
         return pltpu.make_async_remote_copy(
             src_ref=result.at[j, to], dst_ref=back_ref.at[j * n + me],
             send_sem=b_send.at[j, off], recv_sem=b_recv.at[j, off],
@@ -99,11 +118,32 @@
     def mine_out(j):
         return pltpu.make_async_copy(result.at[j, me], back_ref.at[j * n + me], own_out.at[j])
 
+    def signal(semaphore, **to):
+        pl.semaphore_signal(semaphore, inc=1, device_id=to, device_id_type=MESH)
+
     barrier = pltpu.get_barrier_semaphore()
-    for off in range(n - 1, 0, -1):
-        pl.semaphore_signal(barrier, inc=1, device_id={"shard": partner(me, off, n)}, device_id_type=MESH)
-    for off in range(1, k):
-        pl.semaphore_signal(barrier, inc=1, device_id={"model": partner(col, off, k)}, device_id_type=MESH)
+    if early:
+        @pl.when(middle)
+        def _():
+            for off in facing:
+                signal(barrier, shard=partner(me, off, n))
+
+        @pl.when(jnp.logical_not(hub))
+        def _():
+            signal(barrier, shard=0)
+
+        @pl.when(hub)
+        def _():
+            for off in range(1, k):
+                signal(barrier, model=partner(col, off, k))
+            for to in range(1, n):
+                if not n // 2 - 2 <= to <= n // 2 + 1:
+                    signal(barrier, shard=to)
+    else:
+        for off in range(n - 1, 0, -1):
+            signal(barrier, shard=partner(me, off, n))
+        for off in range(1, k):
+            signal(barrier, model=partner(col, off, k))
 
     @pl.loop(0, local)
     def _(j):
@@ -115,28 +155,60 @@
         load_grad(j).wait()
         moved[j] = hold_rate * moved[j] + grad[j]
 
+    def send_facing(j):
+        @pl.when(middle)
+        def _():
+            for off in facing:
+                forward(j, off, partner(me, off, n)).start()
+
     def send(j):
+        for off, to in partners(me, n):
+            if early:
+                @pl.when(jnp.logical_not(jnp.logical_and(middle, off >= n - 2)))
+                def _():
+                    forward(j, off, to).start()
+            else:
+                forward(j, off, to).start()
+        mine_in(j).start()
+
+    step(0)
+    if early:
+        pl.semaphore_wait(barrier, jnp.where(hub, n + k - 2, jnp.where(middle, 2, 1)))
+        send_facing(0)
+    else:
+        pl.semaphore_wait(barrier, n + k - 2)
+
+    @pl.loop(1, local)
+    def _(j):
+        step(j)
+        if early:
+            send_facing(j)
+
+    if early:
+        @pl.when(hub)
+        def _():
+            for off in range(1, k):
+                signal(met, model=partner(col, off, k))
+            pl.semaphore_wait(met, k - 1)
+            for to in range(n - 1, 0, -1):
+                signal(go, shard=to)
+
+        @pl.when(jnp.logical_not(hub))
+        def _():
+            pl.semaphore_wait(go, 1)
+
+    @pl.loop(0, local)
+    def _(j):
+        send(j)
+
+    @pl.loop(0, local)
+    def _(j):
+        store_new(j).start()
+
+    @pl.loop(0, local)
+    def _(j):
         for off in range(1, n):
-            forward(j, off).start()
-        mine_in(j).start()
-
-    step(0)
-    pl.semaphore_wait(barrier, n + k - 2)
-    send(0)
-
-    @pl.loop(1, local)
-    def _(j):
-        step(j)
-        send(j)
-
-    @pl.loop(0, local)
-    def _(j):
-        store_new(j).start()
-
-    @pl.loop(0, local)
-    def _(j):
-        for off in range(1, n):
-            forward(j, off).wait_recv()
+            forward(j, off, partner(me, off, n)).wait_recv()
         mine_in(j).wait()
         x = held[j].reshape(side, wide)
         grams[j, col] = lax.dot_general(
@@ -149,14 +221,14 @@
         for i in range(1, k):
             gram = gram + grams[j, i]
         result[j] = mm(direction(gram), x).reshape(n, rows, wide)
+        for off, to in partners(me, n):
+            backward(j, off, to).start()
+        mine_out(j).start()
+
+    @pl.loop(0, local)
+    def _(j):
         for off in range(1, n):
-            backward(j, off).start()
-        mine_out(j).start()
-
-    @pl.loop(0, local)
-    def _(j):
-        for off in range(1, n):
-            forward(j, off).wait_send()
+            forward(j, off, partner(me, off, n)).wait_send()
         for off in range(1, k):
             share(j, off).wait_send()
         store_new(j).wait()
@@ -165,7 +237,7 @@
     @pl.loop(0, local)
     def _(j):
         for off in range(1, n):
-            backward(j, off).wait()
+            backward(j, off, partner(me, off, n)).wait()
 
 
 def by_kernel(n, k, gradients, momentum):
@@ -187,6 +259,7 @@
             dma((local, k)), dma((local, k)),
             dma((local, n)), dma((local, n)),
             dma((local,)), dma((local,)), dma((local,)),
+            pltpu.SemaphoreType.REGULAR, pltpu.SemaphoreType.REGULAR,
         ],
         compiler_params=pltpu.CompilerParams(
             collective_id=0, has_side_effects=True, vmem_limit_bytes=VMEM_LIMIT),

time: 100 us -> 98.8 us (0.988)
  Pallas kernels: 98.6 us -> 96.9 us
    pallas_call x1, Pallas kernels: 96.5 us -> 94.8 us  [by_kernel(): pl.pallas_call(functools.partial(exchange_kernel, n, k), out_shape=(whole...]
where the time goes in v1:
time: 98.8 us; the launch traced here: 97.6 us
  Pallas kernels  96.9 us (98%)
    pallas_call x1, Pallas kernels, by_kernel(): pl.pallas_call(functools.partial(exchange_kernel, n, k), out_shape=(whole...  94.8 us
    pallas_call x1, Pallas kernels, finish(): pl.pallas_call(functools.partial(finish_kernel, pieces), out_shape=(whole...  2.13 us

profile of v1, /device:TPU:9, one launch (start us, length us, event | category | flops | bytes accessed | tf_op | source)
XLA Modules:
  0.0 97.6 jit_solution(14772052000328125196)
XLA Ops:
  0.6 0.0 copy-start
  0.6 94.8 %shard_map.50 = (f32[32,16,1024]{2,1,0:T(8,128)S(1)}, f32[32,16,1024]{2,1,0:T(8,128)S(1)}) custom-call(f32[32,16,1024]{2,1,0:T(8,128)} %g_ref.1, f32[32,16,1024]{2,1,0:T(8,128)} %m_ref.1), custom_call_target="tpu_custom_call" | custom-call | tf_op jit(solution)/shard_map/pallas_call | solution.py:249
  95.4 0.0 copy-done
  95.4 2.1 %shard_map.51 = (f32[32,16,1024]{2,1,0:T(8,128)}, f32[32,16,1024]{2,1,0:T(8,128)}) custom-call(f32[32,16,1024]{2,1,0:T(8,128)S(1)} %get-tuple-element.4.back_ref, f32[32,16,1024]{2,1,0:T(8,128)S(1)} %copy-done, f32[32,16,1024]{2,1,0:T(8,128)S(1)} %get-tuple-element.5.new_ref), custom_call_target="tpu_custom_call" | custom-call | flops 1048576 | bytes 10485760 | tf_op jit(solution)/shard_map/pallas_call | solution.py:295
Async XLA Ops:
  0.6 94.8 %copy-start = (f32[32,16,1024]{2,1,0:T(8,128)S(1)}, f32[32,16,1024]{2,1,0:T(8,128)}, u32[]{:S(2)}) copy-start(f32[32,16,1024]{2,1,0:T(8,128)} %w_ref.1) | copy-start | bytes 6291460

commit v2 on v1

--- a/solution.py
+++ b/solution.py
@@ -70,9 +70,8 @@
     return found
 
 
-def exchange_kernel(n, k, g_ref, m_ref, back_ref, new_ref, grad, moved, held, result, grams,
-                    l_grad, l_moved, f_send, f_recv, g_send, g_recv, b_send, b_recv,
-                    own_in, own_out, own_new, met, go):
+def exchange_kernel(n, k, g_ref, m_ref, w_ref, done_ref, new_ref, grad, held, weight, result, grams,
+                    l_grad, l_moved, l_weight, f_send, f_recv, g_send, g_recv, b_send, b_recv, met, go):
     me = lax.axis_index("shard")
     col = lax.axis_index("model")
     local, _, rows, wide = held.shape
@@ -89,34 +88,31 @@
         return pltpu.make_async_copy(g_ref.at[chunk(j)], grad.at[j], l_grad.at[j])
 
     def load_moved(j):
-        return pltpu.make_async_copy(m_ref.at[chunk(j)], moved.at[j], l_moved.at[j])
-
-    def store_new(j):
-        return pltpu.make_async_copy(moved.at[j], new_ref.at[chunk(j)], own_new.at[j])
+        return pltpu.make_async_copy(m_ref.at[chunk(j)], new_ref.at[chunk(j)], l_moved.at[j])
+
+    def load_weight():
+        return pltpu.make_async_copy(w_ref, weight, l_weight)
 
     def forward(j, off, to):
         return pltpu.make_async_remote_copy(
-            src_ref=moved.at[j, to], dst_ref=held.at[j, me],
-            send_sem=f_send.at[j, off], recv_sem=f_recv.at[j, off],
+            src_ref=new_ref.at[j * n + to], dst_ref=held.at[j, me],
+            send_sem=f_send, recv_sem=f_recv.at[j],
             device_id={"shard": to}, device_id_type=MESH)
 
     def share(j, off):
         return pltpu.make_async_remote_copy(
             src_ref=grams.at[j, col], dst_ref=grams.at[j, col],
-            send_sem=g_send.at[j, off], recv_sem=g_recv.at[j, off],
+            send_sem=g_send, recv_sem=g_recv.at[j],
             device_id={"model": partner(col, off, k)}, device_id_type=MESH)
 
     def backward(j, off, to):
         return pltpu.make_async_remote_copy(
-            src_ref=result.at[j, to], dst_ref=back_ref.at[j * n + me],
-            send_sem=b_send.at[j, off], recv_sem=b_recv.at[j, off],
+            src_ref=result.at[j, to], dst_ref=done_ref.at[j * n + me],
+            send_sem=b_send, recv_sem=b_recv.at[j],
             device_id={"shard": to}, device_id_type=MESH)
 
-    def mine_in(j):
-        return pltpu.make_async_copy(moved.at[j, me], held.at[j, me], own_in.at[j])
-
-    def mine_out(j):
-        return pltpu.make_async_copy(result.at[j, me], back_ref.at[j * n + me], own_out.at[j])
+    def drain(ref, semaphore):
+        pltpu.make_async_copy(ref, ref, semaphore).wait()
 
     def signal(semaphore, **to):
         pl.semaphore_signal(semaphore, inc=1, device_id=to, device_id_type=MESH)
@@ -153,7 +149,7 @@
     def step(j):
         load_moved(j).wait()
         load_grad(j).wait()
-        moved[j] = hold_rate * moved[j] + grad[j]
+        new_ref[chunk(j)] = hold_rate * new_ref[chunk(j)] + grad[j]
 
     def send_facing(j):
         @pl.when(middle)
@@ -169,7 +165,6 @@
                     forward(j, off, to).start()
             else:
                 forward(j, off, to).start()
-        mine_in(j).start()
 
     step(0)
     if early:
@@ -201,46 +196,39 @@
     def _(j):
         send(j)
 
-    @pl.loop(0, local)
-    def _(j):
-        store_new(j).start()
-
-    @pl.loop(0, local)
-    def _(j):
-        for off in range(1, n):
-            forward(j, off, partner(me, off, n)).wait_recv()
-        mine_in(j).wait()
+    load_weight().start()
+
+    @pl.loop(0, local)
+    def _(j):
+        held[j, me] = new_ref[j * n + me]
+        drain(held.at[j, pl.ds(0, n - 1)], f_recv.at[j])
         x = held[j].reshape(side, wide)
         grams[j, col] = lax.dot_general(
             x, x, (((1,), (1,)), ((), ())), precision=HIGHEST, preferred_element_type=jnp.float32)
         for off in range(1, k):
             share(j, off).start()
-        for off in range(1, k):
-            share(j, off).wait_recv()
+        drain(grams.at[j, pl.ds(0, k - 1)], g_recv.at[j])
         gram = grams[j, 0]
         for i in range(1, k):
             gram = gram + grams[j, i]
         result[j] = mm(direction(gram), x).reshape(n, rows, wide)
         for off, to in partners(me, n):
             backward(j, off, to).start()
-        mine_out(j).start()
-
-    @pl.loop(0, local)
-    def _(j):
-        for off in range(1, n):
-            forward(j, off, partner(me, off, n)).wait_send()
-        for off in range(1, k):
-            share(j, off).wait_send()
-        store_new(j).wait()
-        mine_out(j).wait()
-
-    @pl.loop(0, local)
-    def _(j):
-        for off in range(1, n):
-            backward(j, off, partner(me, off, n)).wait()
-
-
-def by_kernel(n, k, gradients, momentum):
+        done_ref[j * n + me] = result[j, me]
+
+    load_weight().wait()
+
+    @pl.loop(0, local)
+    def _(j):
+        drain(done_ref.at[pl.ds(j * n, n - 1)], b_recv.at[j])
+        done_ref[chunk(j)] = weight[chunk(j)] - learn_rate * done_ref[chunk(j)]
+
+    drain(new_ref.at[pl.ds(0, local * (n - 1))], f_send)
+    drain(grams.at[:, pl.ds(0, k - 1)], g_send)
+    drain(new_ref.at[pl.ds(0, local * (n - 1))], b_send)
+
+
+def by_kernel(n, k, gradients, momentum, weights):
     mats, rows, wide = gradients.shape
     local = mats // n
     side = n * rows
@@ -249,66 +237,53 @@
     return pl.pallas_call(
         functools.partial(exchange_kernel, n, k),
         out_shape=(whole, whole),
-        in_specs=[pl.BlockSpec(memory_space=pltpu.HBM)] * 2,
-        out_specs=[pl.BlockSpec(memory_space=pl.ANY)] * 2,
+        in_specs=[pl.BlockSpec(memory_space=pltpu.HBM)] * 3,
+        out_specs=[pl.BlockSpec(memory_space=pltpu.VMEM)] * 2,
         scratch_shapes=[
-            *[pltpu.VMEM((local, n, rows, wide), jnp.float32)] * 4,
+            *[pltpu.VMEM((local, n, rows, wide), jnp.float32)] * 2,
+            pltpu.VMEM(gradients.shape, jnp.float32),
+            pltpu.VMEM((local, n, rows, wide), jnp.float32),
             pltpu.VMEM((local, k, side, side), jnp.float32),
-            dma((local,)), dma((local,)),
-            dma((local, n)), dma((local, n)),
-            dma((local, k)), dma((local, k)),
-            dma((local, n)), dma((local, n)),
-            dma((local,)), dma((local,)), dma((local,)),
+            dma((local,)), dma((local,)), dma(()),
+            dma(()), dma((local,)),
+            dma(()), dma((local,)),
+            dma(()), dma((local,)),
             pltpu.SemaphoreType.REGULAR, pltpu.SemaphoreType.REGULAR,
         ],
         compiler_params=pltpu.CompilerParams(
             collective_id=0, has_side_effects=True, vmem_limit_bytes=VMEM_LIMIT),
-    )(pltpu.with_memory_space_constraint(gradients, pltpu.HBM), pltpu.with_memory_space_constraint(momentum, pltpu.HBM))
-
-
-def finish_kernel(pieces, back_ref, w_ref, new_ref, out_w, out_new, done, sem_w, sem_new):
-    step = back_ref.shape[0] // pieces
-
-    def part(i):
-        return pl.ds(i * step, step)
-
-    def put_new(i):
-        return pltpu.make_async_copy(new_ref.at[part(i)], out_new.at[part(i)], sem_new.at[i])
-
-    def put_w(i):
-        return pltpu.make_async_copy(done.at[part(i)], out_w.at[part(i)], sem_w.at[i])
-
+    )(*[pltpu.with_memory_space_constraint(a, pltpu.HBM) for a in (gradients, momentum, weights)])
+
+
+def finish_kernel(pieces, done_ref, new_ref, out_w, out_new, semaphores):
+    step = done_ref.shape[0] // pieces
+    copies = []
     for i in range(pieces):
-        put_new(i).start()
-    for i in range(pieces):
-        done[part(i)] = w_ref[part(i)] - learn_rate * back_ref[part(i)]
-        put_w(i).start()
-    for i in range(pieces):
-        put_new(i).wait()
-        put_w(i).wait()
-
-
-def finish(pieces, back, weights, new_momentum):
-    whole = jax.ShapeDtypeStruct(back.shape, jnp.float32)
-    hold = pl.BlockSpec(memory_space=pltpu.VMEM)
-    leave = pl.BlockSpec(memory_space=pl.ANY)
+        part = pl.ds(i * step, step)
+        for source, target in ((done_ref, out_w), (new_ref, out_new)):
+            copies.append(pltpu.make_async_copy(source.at[part], target.at[part], semaphores.at[len(copies)]))
+    for copy in copies:
+        copy.start()
+    for copy in copies:
+        copy.wait()
+
+
+def finish(pieces, done, new_momentum):
+    whole = jax.ShapeDtypeStruct(done.shape, jnp.float32)
     return pl.pallas_call(
         functools.partial(finish_kernel, pieces),
         out_shape=(whole, whole),
-        in_specs=[hold, hold, leave],
-        out_specs=[leave, leave],
-        scratch_shapes=[
-            pltpu.VMEM(back.shape, jnp.float32),
-            pltpu.SemaphoreType.DMA((pieces,)), pltpu.SemaphoreType.DMA((pieces,)),
-        ],
+        in_specs=[pl.BlockSpec(memory_space=pltpu.VMEM)] * 2,
+        out_specs=[pl.BlockSpec(memory_space=pl.ANY)] * 2,
+        scratch_shapes=[pltpu.SemaphoreType.DMA((2 * pieces,))],
         compiler_params=pltpu.CompilerParams(vmem_limit_bytes=FINISH_LIMIT),
-        cost_estimate=pl.CostEstimate(flops=2 * back.size, bytes_accessed=20 * back.size, transcendentals=0),
-    )(back, weights, new_momentum)
+        cost_estimate=pl.CostEstimate(flops=2 * done.size, bytes_accessed=16 * done.size, transcendentals=0),
+    )(done, new_momentum)
 
 
 def on_device(n, k, gradients, momentum, weights):
-    back, new_momentum = by_kernel(n, k, gradients, momentum)
-    return tuple(finish(n, back, weights, new_momentum))
+    done, new_momentum = by_kernel(n, k, gradients, momentum, weights)
+    return tuple(finish(2, done, new_momentum))
 
 
 def solution(mesh):

time: 98.8 us -> 97.3 us (0.985)
  Pallas kernels: 96.9 us -> 95.3 us
    pallas_call x1, Pallas kernels: 94.8 us -> 93.2 us  [by_kernel(): pl.pallas_call(functools.partial(exchange_kernel, n, k), out_shape=(whole...]
where the time goes in v2:
time: 97.3 us; the launch traced here: 95.9 us
  Pallas kernels  95.3 us (98%)
    pallas_call x1, Pallas kernels, by_kernel(): pl.pallas_call(functools.partial(exchange_kernel, n, k), out_shape=(whole...  93.2 us
    pallas_call x1, Pallas kernels, finish(): pl.pallas_call(functools.partial(finish_kernel, pieces), out_shape=(whole...  2.04 us

profile of v2, /device:TPU:9, one launch (start us, length us, event | category | flops | bytes accessed | tf_op | source)
XLA Modules:
  0.0 95.9 jit_solution(17521710705724947792)
XLA Ops:
  0.6 93.2 %shard_map.50 = (f32[32,16,1024]{2,1,0:T(8,128)S(1)}, f32[32,16,1024]{2,1,0:T(8,128)S(1)}) custom-call(f32[32,16,1024]{2,1,0:T(8,128)} %g_ref.1, f32[32,16,1024]{2,1,0:T(8,128)} %m_ref.1, f32[32,16,1024]{2,1,0:T(8,128)} %w_ref.1), custom_call_target="tpu_custom_call" | custom-call | tf_op jit(solution)/shard_map/pallas_call | solution.py:237
  93.9 2.0 %shard_map.51 = (f32[32,16,1024]{2,1,0:T(8,128)}, f32[32,16,1024]{2,1,0:T(8,128)}) custom-call(f32[32,16,1024]{2,1,0:T(8,128)S(1)} %get-tuple-element.4.done_ref, f32[32,16,1024]{2,1,0:T(8,128)S(1)} %get-tuple-element.5.new_ref), custom_call_target="tpu_custom_call" | custom-call | flops 1048576 | bytes 8388608 | tf_op jit(solution)/shard_map/pallas_call | solution.py:273

commit v3 on v2

--- a/solution.py
+++ b/solution.py
@@ -70,8 +70,27 @@
     return found
 
 
-def exchange_kernel(n, k, g_ref, m_ref, w_ref, done_ref, new_ref, grad, held, weight, result, grams,
-                    l_grad, l_moved, l_weight, f_send, f_recv, g_send, g_recv, b_send, b_recv, met, go):
+def across(me, n, upper):
+    if n & (n - 1) or n < 8:
+        return []
+    quarter = n // 4
+    shift = lax.rem(me // quarter + upper, 2) * quarter
+    start = me // (2 * quarter) * -2 * quarter + (2 * quarter)
+    return [(off + shift, start + upper * quarter + inner_place(me, off, quarter))
+            for off in range(3 * quarter - 1, 2 * quarter - 1, -1)]
+
+
+def inner_place(me, off, quarter):
+    return partner(lax.rem(me, quarter), off % quarter, quarter)
+
+
+def within(me, n):
+    top = n - 1 if n & (n - 1) or n < 8 else n // 2 - 1
+    return [(off, partner(me, off, n)) for off in range(top, 0, -1)]
+
+
+def exchange_kernel(n, k, g_ref, m_ref, w_ref, done_ref, new_ref, grad, held, weight, result, grams, first,
+                    l_grad, l_moved, l_weight, l_first, f_send, f_recv, g_send, g_recv, b_send, b_recv, near, met, go):
     me = lax.axis_index("shard")
     col = lax.axis_index("model")
     local, _, rows, wide = held.shape
@@ -79,7 +98,8 @@
     early = n >= 8 and n & (n - 1) == 0
     middle = jnp.logical_and(me >= n // 2 - 2, me <= n // 2 + 1)
     hub = me == 0
-    facing = (n - 1, n - 2)
+    across_off, opposite_off = n - 1, n - 2
+    opposite = partner(me, opposite_off, n)
 
     def chunk(j):
         return pl.ds(j * n, n)
@@ -90,12 +110,15 @@
     def load_moved(j):
         return pltpu.make_async_copy(m_ref.at[chunk(j)], new_ref.at[chunk(j)], l_moved.at[j])
 
+    def load_first(i, ref):
+        return pltpu.make_async_copy(ref.at[opposite], first.at[i], l_first.at[i])
+
     def load_weight():
         return pltpu.make_async_copy(w_ref, weight, l_weight)
 
-    def forward(j, off, to):
+    def forward(j, off, to, source=None):
         return pltpu.make_async_remote_copy(
-            src_ref=new_ref.at[j * n + to], dst_ref=held.at[j, me],
+            src_ref=new_ref.at[j * n + to] if source is None else source, dst_ref=held.at[j, me],
             send_sem=f_send, recv_sem=f_recv.at[j],
             device_id={"shard": to}, device_id_type=MESH)
 
@@ -121,8 +144,8 @@
     if early:
         @pl.when(middle)
         def _():
-            for off in facing:
-                signal(barrier, shard=partner(me, off, n))
+            signal(barrier, shard=opposite)
+            signal(barrier, shard=partner(me, 1, n))
 
         @pl.when(jnp.logical_not(hub))
         def _():
@@ -141,6 +164,10 @@
         for off in range(1, k):
             signal(barrier, model=partner(col, off, k))
 
+    if early:
+        load_first(0, m_ref).start()
+        load_first(1, g_ref).start()
+
     @pl.loop(0, local)
     def _(j):
         load_moved(j).start()
@@ -150,12 +177,6 @@
         load_moved(j).wait()
         load_grad(j).wait()
         new_ref[chunk(j)] = hold_rate * new_ref[chunk(j)] + grad[j]
-
-    def send_facing(j):
-        @pl.when(middle)
-        def _():
-            for off in facing:
-                forward(j, off, partner(me, off, n)).start()
 
     def send(j):
         for off, to in partners(me, n):
@@ -166,18 +187,41 @@
             else:
                 forward(j, off, to).start()
 
-    step(0)
     if early:
+        load_first(0, m_ref).wait()
+        load_first(1, g_ref).wait()
+        first[0] = hold_rate * first[0] + first[1]
         pl.semaphore_wait(barrier, jnp.where(hub, n + k - 2, jnp.where(middle, 2, 1)))
-        send_facing(0)
+
+        @pl.when(middle)
+        def _():
+            forward(0, opposite_off, opposite, first.at[0]).start()
+            signal(near, shard=partner(me, 1, n))
+
+        @pl.loop(1, local)
+        def _(j):
+            step(j)
+
+            @pl.when(middle)
+            def _():
+                forward(j, opposite_off, opposite).start()
+
+        step(0)
+
+        @pl.when(middle)
+        def _():
+            pl.semaphore_wait(near, 1)
+
+            @pl.loop(0, local)
+            def _(j):
+                forward(j, across_off, partner(me, across_off, n)).start()
     else:
+        step(0)
         pl.semaphore_wait(barrier, n + k - 2)
 
-    @pl.loop(1, local)
-    def _(j):
-        step(j)
-        if early:
-            send_facing(j)
+        @pl.loop(1, local)
+        def _(j):
+            step(j)
 
     if early:
         @pl.when(hub)
@@ -212,7 +256,17 @@
         for i in range(1, k):
             gram = gram + grams[j, i]
         result[j] = mm(direction(gram), x).reshape(n, rows, wide)
-        for off, to in partners(me, n):
+        for off, to in across(me, n, 0):
+            backward(j, off, to).start()
+
+        @pl.when(jnp.logical_or(j < local - 2, j == local - 1))
+        def _():
+            @pl.loop(jnp.where(j == local - 1, max(local - 2, 0), j), j + 1)
+            def _(i):
+                for off, to in across(me, n, 1):
+                    backward(i, off, to).start()
+
+        for off, to in within(me, n):
             backward(j, off, to).start()
         done_ref[j * n + me] = result[j, me]
 
@@ -244,11 +298,12 @@
             pltpu.VMEM(gradients.shape, jnp.float32),
             pltpu.VMEM((local, n, rows, wide), jnp.float32),
             pltpu.VMEM((local, k, side, side), jnp.float32),
-            dma((local,)), dma((local,)), dma(()),
+            pltpu.VMEM((2, rows, wide), jnp.float32),
+            dma((local,)), dma((local,)), dma(()), dma((2,)),
             dma(()), dma((local,)),
             dma(()), dma((local,)),
             dma(()), dma((local,)),
-            pltpu.SemaphoreType.REGULAR, pltpu.SemaphoreType.REGULAR,
+            *[pltpu.SemaphoreType.REGULAR] * 3,
         ],
         compiler_params=pltpu.CompilerParams(
             collective_id=0, has_side_effects=True, vmem_limit_bytes=VMEM_LIMIT),

time: 97.3 us -> 96.7 us (level)
  no operation moved by 1% of the time
where the time goes in v3:
time: 96.7 us; the launch traced here: 95.6 us
  Pallas kernels  95 us (98%)
    pallas_call x1, Pallas kernels, by_kernel(): pl.pallas_call(functools.partial(exchange_kernel, n, k), out_shape=(whole...  92.9 us
    pallas_call x1, Pallas kernels, finish(): pl.pallas_call(functools.partial(finish_kernel, pieces), out_shape=(whole...  2.04 us

profile of v3, /device:TPU:9, one launch (start us, length us, event | category | flops | bytes accessed | tf_op | source)
XLA Modules:
  0.0 95.6 jit_solution(12264423394696666959)
XLA Ops:
  0.6 92.9 %shard_map.50 = (f32[32,16,1024]{2,1,0:T(8,128)S(1)}, f32[32,16,1024]{2,1,0:T(8,128)S(1)}) custom-call(f32[32,16,1024]{2,1,0:T(8,128)} %g_ref.1, f32[32,16,1024]{2,1,0:T(8,128)} %m_ref.1, f32[32,16,1024]{2,1,0:T(8,128)} %w_ref.1), custom_call_target="tpu_custom_call" | custom-call | tf_op jit(solution)/shard_map/pallas_call | solution.py:291
  93.6 2.0 %shard_map.51 = (f32[32,16,1024]{2,1,0:T(8,128)}, f32[32,16,1024]{2,1,0:T(8,128)}) custom-call(f32[32,16,1024]{2,1,0:T(8,128)S(1)} %get-tuple-element.4.done_ref, f32[32,16,1024]{2,1,0:T(8,128)S(1)} %get-tuple-element.5.new_ref), custom_call_target="tpu_custom_call" | custom-call | flops 1048576 | bytes 8388608 | tf_op jit(solution)/shard_map/pallas_call | solution.py:328

commit v4 on v3

--- a/solution.py
+++ b/solution.py
@@ -97,9 +97,12 @@
     side = n * rows
     early = n >= 8 and n & (n - 1) == 0
     middle = jnp.logical_and(me >= n // 2 - 2, me <= n // 2 + 1)
+    lower = jnp.logical_and(middle, me < n // 2)
     hub = me == 0
     across_off, opposite_off = n - 1, n - 2
     opposite = partner(me, opposite_off, n)
+    late = lax.rem(col, 2) == 1
+    prompt = jnp.logical_and(middle, jnp.logical_not(late))
 
     def chunk(j):
         return pl.ds(j * n, n)
@@ -142,9 +145,15 @@
 
     barrier = pltpu.get_barrier_semaphore()
     if early:
+        load_first(0, m_ref).start()
+        load_first(1, g_ref).start()
+
         @pl.when(middle)
         def _():
             signal(barrier, shard=opposite)
+
+        @pl.when(lower)
+        def _():
             signal(barrier, shard=partner(me, 1, n))
 
         @pl.when(jnp.logical_not(hub))
@@ -164,10 +173,6 @@
         for off in range(1, k):
             signal(barrier, model=partner(col, off, k))
 
-    if early:
-        load_first(0, m_ref).start()
-        load_first(1, g_ref).start()
-
     @pl.loop(0, local)
     def _(j):
         load_moved(j).start()
@@ -191,18 +196,22 @@
         load_first(0, m_ref).wait()
         load_first(1, g_ref).wait()
         first[0] = hold_rate * first[0] + first[1]
-        pl.semaphore_wait(barrier, jnp.where(hub, n + k - 2, jnp.where(middle, 2, 1)))
+        pl.semaphore_wait(barrier, jnp.where(hub, n + k - 2, jnp.where(lower, 2, 1)))
 
         @pl.when(middle)
         def _():
             forward(0, opposite_off, opposite, first.at[0]).start()
+
+        @pl.when(lower)
+        def _():
             signal(near, shard=partner(me, 1, n))
+            signal(near, shard=opposite)
 
         @pl.loop(1, local)
         def _(j):
             step(j)
 
-            @pl.when(middle)
+            @pl.when(jnp.logical_and(middle, jnp.logical_or(jnp.logical_not(late), j < local - 1)))
             def _():
                 forward(j, opposite_off, opposite).start()
 
@@ -212,6 +221,8 @@
         def _():
             pl.semaphore_wait(near, 1)
 
+        @pl.when(prompt)
+        def _():
             @pl.loop(0, local)
             def _(j):
                 forward(j, across_off, partner(me, across_off, n)).start()
@@ -235,6 +246,17 @@
         @pl.when(jnp.logical_not(hub))
         def _():
             pl.semaphore_wait(go, 1)
+
+    if early:
+        @pl.when(jnp.logical_and(middle, late))
+        def _():
+            @pl.loop(max(local - 1, 1), local)
+            def _(j):
+                forward(j, opposite_off, opposite).start()
+
+            @pl.loop(0, local)
+            def _(j):
+                forward(j, across_off, partner(me, across_off, n)).start()
 
     @pl.loop(0, local)
     def _(j):

time: 96.7 us -> 96.6 us (level)
  no operation moved by 1% of the time
where the time goes in v4:
time: 96.6 us; the launch traced here: 96.4 us
  Pallas kernels  95.8 us (99%)
    pallas_call x1, Pallas kernels, by_kernel(): pl.pallas_call(functools.partial(exchange_kernel, n, k), out_shape=(whole...  93.7 us
    pallas_call x1, Pallas kernels, finish(): pl.pallas_call(functools.partial(finish_kernel, pieces), out_shape=(whole...  2.04 us

profile of v4, /device:TPU:9, one launch (start us, length us, event | category | flops | bytes accessed | tf_op | source)
XLA Modules:
  0.0 96.4 jit_solution(18291158819259897364)
XLA Ops:
  0.6 93.7 %shard_map.50 = (f32[32,16,1024]{2,1,0:T(8,128)S(1)}, f32[32,16,1024]{2,1,0:T(8,128)S(1)}) custom-call(f32[32,16,1024]{2,1,0:T(8,128)} %g_ref.1, f32[32,16,1024]{2,1,0:T(8,128)} %m_ref.1, f32[32,16,1024]{2,1,0:T(8,128)} %w_ref.1), custom_call_target="tpu_custom_call" | custom-call | tf_op jit(solution)/shard_map/pallas_call | solution.py:313
  94.4 2.0 %shard_map.51 = (f32[32,16,1024]{2,1,0:T(8,128)}, f32[32,16,1024]{2,1,0:T(8,128)}) custom-call(f32[32,16,1024]{2,1,0:T(8,128)S(1)} %get-tuple-element.4.done_ref, f32[32,16,1024]{2,1,0:T(8,128)S(1)} %get-tuple-element.5.new_ref), custom_call_target="tpu_custom_call" | custom-call | flops 1048576 | bytes 8388608 | tf_op jit(solution)/shard_map/pallas_call | solution.py:350

commit v5 on v4

--- a/solution.py
+++ b/solution.py
@@ -89,8 +89,8 @@
     return [(off, partner(me, off, n)) for off in range(top, 0, -1)]
 
 
-def exchange_kernel(n, k, g_ref, m_ref, w_ref, done_ref, new_ref, grad, held, weight, result, grams, first,
-                    l_grad, l_moved, l_weight, l_first, f_send, f_recv, g_send, g_recv, b_send, b_recv, near, met, go):
+def exchange_kernel(n, k, g_ref, m_ref, w_ref, done_ref, new_ref, pair, held, weight, result, grams, first,
+                    l_pair, l_weight, l_first, f_send, f_recv, g_send, g_recv, b_send, b_recv, near, go):
     me = lax.axis_index("shard")
     col = lax.axis_index("model")
     local, _, rows, wide = held.shape
@@ -108,13 +108,13 @@
         return pl.ds(j * n, n)
 
     def load_grad(j):
-        return pltpu.make_async_copy(g_ref.at[chunk(j)], grad.at[j], l_grad.at[j])
+        return pltpu.make_async_copy(g_ref.at[chunk(j)], pair.at[j, 1], l_pair.at[j])
 
     def load_moved(j):
-        return pltpu.make_async_copy(m_ref.at[chunk(j)], new_ref.at[chunk(j)], l_moved.at[j])
+        return pltpu.make_async_copy(m_ref.at[chunk(j)], pair.at[j, 0], l_pair.at[j])
 
     def load_first(i, ref):
-        return pltpu.make_async_copy(ref.at[opposite], first.at[i], l_first.at[i])
+        return pltpu.make_async_copy(ref.at[opposite], first.at[i], l_first)
 
     def load_weight():
         return pltpu.make_async_copy(w_ref, weight, l_weight)
@@ -128,13 +128,13 @@
     def share(j, off):
         return pltpu.make_async_remote_copy(
             src_ref=grams.at[j, col], dst_ref=grams.at[j, col],
-            send_sem=g_send, recv_sem=g_recv.at[j],
+            send_sem=g_send, recv_sem=g_recv.at[lax.rem(j, 2)],
             device_id={"model": partner(col, off, k)}, device_id_type=MESH)
 
     def backward(j, off, to):
         return pltpu.make_async_remote_copy(
             src_ref=result.at[j, to], dst_ref=done_ref.at[j * n + me],
-            send_sem=b_send, recv_sem=b_recv.at[j],
+            send_sem=b_send, recv_sem=b_recv.at[j // max(local - 1, 1)],
             device_id={"shard": to}, device_id_type=MESH)
 
     def drain(ref, semaphore):
@@ -179,9 +179,8 @@
         load_grad(j).start()
 
     def step(j):
-        load_moved(j).wait()
-        load_grad(j).wait()
-        new_ref[chunk(j)] = hold_rate * new_ref[chunk(j)] + grad[j]
+        drain(pair.at[j], l_pair.at[j])
+        new_ref[chunk(j)] = hold_rate * pair[j, 0] + pair[j, 1]
 
     def send(j):
         for off, to in partners(me, n):
@@ -193,8 +192,7 @@
                 forward(j, off, to).start()
 
     if early:
-        load_first(0, m_ref).wait()
-        load_first(1, g_ref).wait()
+        drain(first, l_first)
         first[0] = hold_rate * first[0] + first[1]
         pl.semaphore_wait(barrier, jnp.where(hub, n + k - 2, jnp.where(lower, 2, 1)))
 
@@ -238,8 +236,8 @@
         @pl.when(hub)
         def _():
             for off in range(1, k):
-                signal(met, model=partner(col, off, k))
-            pl.semaphore_wait(met, k - 1)
+                signal(go, model=partner(col, off, k))
+            pl.semaphore_wait(go, k - 1)
             for to in range(n - 1, 0, -1):
                 signal(go, shard=to)
 
@@ -273,7 +271,7 @@
             x, x, (((1,), (1,)), ((), ())), precision=HIGHEST, preferred_element_type=jnp.float32)
         for off in range(1, k):
             share(j, off).start()
-        drain(grams.at[j, pl.ds(0, k - 1)], g_recv.at[j])
+        drain(grams.at[j, pl.ds(0, k - 1)], g_recv.at[lax.rem(j, 2)])
         gram = grams[j, 0]
         for i in range(1, k):
             gram = gram + grams[j, i]
@@ -294,10 +292,19 @@
 
     load_weight().wait()
 
-    @pl.loop(0, local)
+    def subtract(j):
+        done_ref[chunk(j)] = weight[chunk(j)] - learn_rate * done_ref[chunk(j)]
+
+    before = max(local - 1, 1)
+    drain(done_ref.at[pl.ds(0, before * (n - 1))], b_recv.at[0])
+
+    @pl.loop(0, before)
     def _(j):
-        drain(done_ref.at[pl.ds(j * n, n - 1)], b_recv.at[j])
-        done_ref[chunk(j)] = weight[chunk(j)] - learn_rate * done_ref[chunk(j)]
+        subtract(j)
+
+    if before < local:
+        drain(done_ref.at[pl.ds(0, n - 1)], b_recv.at[1])
+        subtract(before)
 
     drain(new_ref.at[pl.ds(0, local * (n - 1))], f_send)
     drain(grams.at[:, pl.ds(0, k - 1)], g_send)
@@ -316,16 +323,17 @@
         in_specs=[pl.BlockSpec(memory_space=pltpu.HBM)] * 3,
         out_specs=[pl.BlockSpec(memory_space=pltpu.VMEM)] * 2,
         scratch_shapes=[
-            *[pltpu.VMEM((local, n, rows, wide), jnp.float32)] * 2,
+            pltpu.VMEM((local, 2, n, rows, wide), jnp.float32),
+            pltpu.VMEM((local, n, rows, wide), jnp.float32),
             pltpu.VMEM(gradients.shape, jnp.float32),
             pltpu.VMEM((local, n, rows, wide), jnp.float32),
             pltpu.VMEM((local, k, side, side), jnp.float32),
             pltpu.VMEM((2, rows, wide), jnp.float32),
-            dma((local,)), dma((local,)), dma(()), dma((2,)),
+            dma((local,)), dma(()), dma(()),
             dma(()), dma((local,)),
-            dma(()), dma((local,)),
-            dma(()), dma((local,)),
-            *[pltpu.SemaphoreType.REGULAR] * 3,
+            dma(()), dma((2,)),
+            dma(()), dma((2,)),
+            *[pltpu.SemaphoreType.REGULAR] * 2,
         ],
         compiler_params=pltpu.CompilerParams(
             collective_id=0, has_side_effects=True, vmem_limit_bytes=VMEM_LIMIT),

time: 96.6 us -> 96.5 us (level)
  no operation moved by 1% of the time
where the time goes in v5:
time: 96.5 us; the launch traced here: 96.3 us
  Pallas kernels  95.7 us (99%)
    pallas_call x1, Pallas kernels, by_kernel(): pl.pallas_call(functools.partial(exchange_kernel, n, k), out_shape=(whole...  93.6 us
    pallas_call x1, Pallas kernels, finish(): pl.pallas_call(functools.partial(finish_kernel, pieces), out_shape=(whole...  2.04 us

profile of v5, /device:TPU:9, one launch (start us, length us, event | category | flops | bytes accessed | tf_op | source)
XLA Modules:
  0.0 96.3 jit_solution(16348760291969192971)
XLA Ops:
  0.6 93.6 %shard_map.50 = (f32[32,16,1024]{2,1,0:T(8,128)S(1)}, f32[32,16,1024]{2,1,0:T(8,128)S(1)}) custom-call(f32[32,16,1024]{2,1,0:T(8,128)} %g_ref.1, f32[32,16,1024]{2,1,0:T(8,128)} %m_ref.1, f32[32,16,1024]{2,1,0:T(8,128)} %w_ref.1), custom_call_target="tpu_custom_call" | custom-call | tf_op jit(solution)/shard_map/pallas_call | solution.py:320
  94.3 2.0 %shard_map.51 = (f32[32,16,1024]{2,1,0:T(8,128)}, f32[32,16,1024]{2,1,0:T(8,128)}) custom-call(f32[32,16,1024]{2,1,0:T(8,128)S(1)} %get-tuple-element.4.done_ref, f32[32,16,1024]{2,1,0:T(8,128)S(1)} %get-tuple-element.5.new_ref), custom_call_target="tpu_custom_call" | custom-call | flops 1048576 | bytes 8388608 | tf_op jit(solution)/shard_map/pallas_call | solution.py:358

commit v6 on v5

--- a/solution.py
+++ b/solution.py
@@ -340,27 +340,23 @@
     )(*[pltpu.with_memory_space_constraint(a, pltpu.HBM) for a in (gradients, momentum, weights)])
 
 
-def finish_kernel(pieces, done_ref, new_ref, out_w, out_new, semaphores):
-    step = done_ref.shape[0] // pieces
-    copies = []
-    for i in range(pieces):
-        part = pl.ds(i * step, step)
-        for source, target in ((done_ref, out_w), (new_ref, out_new)):
-            copies.append(pltpu.make_async_copy(source.at[part], target.at[part], semaphores.at[len(copies)]))
-    for copy in copies:
-        copy.start()
-    for copy in copies:
-        copy.wait()
-
-
-def finish(pieces, done, new_momentum):
+def finish_kernel(done_ref, new_ref, out_w, out_new, semaphores):
+    put_new = pltpu.make_async_copy(new_ref, out_new, semaphores.at[0])
+    put_w = pltpu.make_async_copy(done_ref, out_w, semaphores.at[1])
+    put_new.start()
+    put_w.start()
+    put_new.wait()
+    put_w.wait()
+
+
+def finish(done, new_momentum):
     whole = jax.ShapeDtypeStruct(done.shape, jnp.float32)
     return pl.pallas_call(
-        functools.partial(finish_kernel, pieces),
+        finish_kernel,
         out_shape=(whole, whole),
         in_specs=[pl.BlockSpec(memory_space=pltpu.VMEM)] * 2,
         out_specs=[pl.BlockSpec(memory_space=pl.ANY)] * 2,
-        scratch_shapes=[pltpu.SemaphoreType.DMA((2 * pieces,))],
+        scratch_shapes=[pltpu.SemaphoreType.DMA((2,))],
         compiler_params=pltpu.CompilerParams(vmem_limit_bytes=FINISH_LIMIT),
         cost_estimate=pl.CostEstimate(flops=2 * done.size, bytes_accessed=16 * done.size, transcendentals=0),
     )(done, new_momentum)
@@ -368,7 +364,7 @@
 
 def on_device(n, k, gradients, momentum, weights):
     done, new_momentum = by_kernel(n, k, gradients, momentum, weights)
-    return tuple(finish(2, done, new_momentum))
+    return tuple(finish(done, new_momentum))
 
 
 def solution(mesh):

time: 96.5 us -> 96.5 us (level)
  no operation moved by 1% of the time
where the time goes in v6:
time: 96.5 us; the launch traced here: 96.3 us
  Pallas kernels  95.7 us (99%)
    pallas_call x1, Pallas kernels, by_kernel(): pl.pallas_call(functools.partial(exchange_kernel, n, k), out_shape=(whole...  93.6 us
    pallas_call x1, Pallas kernels, finish(): pl.pallas_call(finish_kernel, out_shape=(whole, whole), in_specs=[pl.Bloc...  2.03 us

profile of v6, /device:TPU:9, one launch (start us, length us, event | category | flops | bytes accessed | tf_op | source)
XLA Modules:
  0.0 96.3 jit_solution(18172040736562868916)
XLA Ops:
  0.6 93.6 %shard_map.50 = (f32[32,16,1024]{2,1,0:T(8,128)S(1)}, f32[32,16,1024]{2,1,0:T(8,128)S(1)}) custom-call(f32[32,16,1024]{2,1,0:T(8,128)} %g_ref.1, f32[32,16,1024]{2,1,0:T(8,128)} %m_ref.1, f32[32,16,1024]{2,1,0:T(8,128)} %w_ref.1), custom_call_target="tpu_custom_call" | custom-call | tf_op jit(solution)/shard_map/pallas_call | solution.py:320
  94.3 2.0 %shard_map.51 = (f32[32,16,1024]{2,1,0:T(8,128)}, f32[32,16,1024]{2,1,0:T(8,128)}) custom-call(f32[32,16,1024]{2,1,0:T(8,128)S(1)} %get-tuple-element.4.done_ref, f32[32,16,1024]{2,1,0:T(8,128)S(1)} %get-tuple-element.5.new_ref), custom_call_target="tpu_custom_call" | custom-call | flops 1048576 | bytes 8388608 | tf_op jit(solution)/shard_map/pallas_call | solution.py:354

commit v7 on v6

--- a/solution.py
+++ b/solution.py
@@ -279,11 +279,16 @@
         for off, to in across(me, n, 0):
             backward(j, off, to).start()
 
-        @pl.when(jnp.logical_or(j < local - 2, j == local - 1))
-        def _():
-            @pl.loop(jnp.where(j == local - 1, max(local - 2, 0), j), j + 1)
-            def _(i):
-                for off, to in across(me, n, 1):
+        @pl.when(j < local - 2)
+        def _():
+            for off, to in across(me, n, 1):
+                backward(j, off, to).start()
+
+        @pl.when(j == local - 1)
+        def _():
+            for off, to in across(me, n, 1):
+                @pl.loop(max(local - 2, 0), local)
+                def _(i):
                     backward(i, off, to).start()
 
         for off, to in within(me, n):

time: 96.5 us -> 96.2 us (level)
  no operation moved by 1% of the time
where the time goes in v7:
time: 96.2 us; the launch traced here: 96.1 us
  Pallas kernels  95.4 us (99%)
    pallas_call x1, Pallas kernels, by_kernel(): pl.pallas_call(functools.partial(exchange_kernel, n, k), out_shape=(whole...  93.4 us
    pallas_call x1, Pallas kernels, finish(): pl.pallas_call(finish_kernel, out_shape=(whole, whole), in_specs=[pl.Bloc...  2.03 us

profile of v7, /device:TPU:9, one launch (start us, length us, event | category | flops | bytes accessed | tf_op | source)
XLA Modules:
  0.0 96.1 jit_solution(157538856487578534)
XLA Ops:
  0.6 93.4 %shard_map.50 = (f32[32,16,1024]{2,1,0:T(8,128)S(1)}, f32[32,16,1024]{2,1,0:T(8,128)S(1)}) custom-call(f32[32,16,1024]{2,1,0:T(8,128)} %g_ref.1, f32[32,16,1024]{2,1,0:T(8,128)} %m_ref.1, f32[32,16,1024]{2,1,0:T(8,128)} %w_ref.1), custom_call_target="tpu_custom_call" | custom-call | tf_op jit(solution)/shard_map/pallas_call | solution.py:325
  94.0 2.0 %shard_map.51 = (f32[32,16,1024]{2,1,0:T(8,128)}, f32[32,16,1024]{2,1,0:T(8,128)}) custom-call(f32[32,16,1024]{2,1,0:T(8,128)S(1)} %get-tuple-element.4.done_ref, f32[32,16,1024]{2,1,0:T(8,128)S(1)} %get-tuple-element.5.new_ref), custom_call_target="tpu_custom_call" | custom-call | flops 1048576 | bytes 8388608 | tf_op jit(solution)/shard_map/pallas_call | solution.py:359
